TPU v7x, 512 devices: a whole 4x8x8 slice. The times are simulated.
512 devices in a mesh: seq: 32 (over x, y), chan: 8 (over z), dp: 2 (over core).
Axes of the slice: x: 4, y: 8, z: 8, core: 2. Of those that a mesh axis runs over, the one named last changes fastest.
Arguments:
- ssm_input: bfloat16 [2, 4096, 4096], P('dp', 'seq', 'chan'), may hold values from -6 to 6
- gate_z: bfloat16 [2, 4096, 4096], P('dp', 'seq', 'chan'), may hold values from -6 to 6
- b_proj: bfloat16 [2, 4096, 128], P('dp', 'seq'), may hold values from -0.52734375 to 0.52734375
- c_proj: bfloat16 [2, 4096, 128], P('dp', 'seq'), may hold values from -6 to 6
- step_size: float32 [2, 4096, 64], P('dp', 'seq', 'chan'), may hold values from 0.02 to 0.2
- log_decay: float32 [2, 4096, 64], P('dp', 'seq', 'chan'), may hold values from -1 to 0, as said below
- skip_d: float32 [64], P('chan'), may hold values from 0.5 to 1.5
- norm_gain: float32 [4096], P('chan'), may hold values from 0.5 to 1.5
- w_out: bfloat16 [4096, 2048], P('chan'), may hold values from -0.09375 to 0.09375
- d_out: bfloat16 [2, 4096, 2048], P('dp', 'seq', 'chan'), may hold values from -6 to 6
- game_lengths: int32 [2, 4], P('dp'), may hold values from 1 to 2048, 4096 in all within a row
Outputs:
- out: bfloat16 [2, 4096, 2048], P('dp', 'seq', 'chan')
- grad_x: bfloat16 [2, 4096, 4096], P('dp', 'seq', 'chan')
- grad_gain: float32 [4096], P('chan')
- grad_skip: float32 [64], P('chan')
Inputs may be any that keep to these rules, and one draw needn't show every extreme that they name: `game_lengths`: each row's 4 game lengths sum to 4096, and the longest is exactly 2048. `log_decay`: a log decay per position and head.
All inputs are finite; a program needn't handle non-finite values.
Results may differ from a plain program's by a relative error of at most 0.017.
Values may be sent and summed in bfloat16 or wider, within the bound.
A program may use at most 64 MiB of HBM per device.

v0:
```python
import jax
import jax.numpy as jnp
from jax import lax
from jax.sharding import Mesh
from jax.sharding import PartitionSpec as P

SEQ = ("seq_0", "seq_1")
SEQ_DP = ("seq_0", "seq_1", "dp")
NORM_EPS = 1e-05


def filled_with(value, identity):
    return jax.tree.map(
        lambda part, zero: jnp.zeros_like(part) + jnp.asarray(zero, part.dtype), value, identity
    )


def prefix_by_axis(value, axes, combine, identity, reverse):
    before = start = filled_with(value, identity)
    so_far = value
    for axis in reversed(axes):
        length, mine = (lax.axis_size(axis), lax.axis_index(axis))
        pieces = jax.tree.map(
            lambda part, kind: lax.all_gather(part.astype(kind), axis),
            so_far,
            (jnp.bfloat16, jnp.bfloat16),
        )
        inside, so_far = (start, start)
        for k in reversed(range(length)) if reverse else range(length):
            passed = k > mine if reverse else k < mine
            so_far = combine(
                so_far, jax.tree.map(lambda part, own: part[k].astype(own.dtype), pieces, value)
            )
            inside = jax.tree.map(lambda new, old: jnp.where(passed, new, old), so_far, inside)
        before = combine(inside, before)
    return before


def in_blocks(value, dim, length):
    lengths = value.shape
    pieces = value.reshape(*lengths[:dim], length, lengths[dim] // length, *lengths[dim + 1 :])
    return jnp.moveaxis(pieces, dim, 0)


def sent_and_summed(value, axis, dim):
    length = lax.axis_size(axis)
    pieces = lax.all_to_all(in_blocks(value, dim, length), axis, 0, 0, tiled=True)
    return jnp.sum(pieces.astype(jnp.float32), axis=0)


def copy_for_each(value, axis):
    length = lax.axis_size(axis)
    return lax.all_to_all(
        jnp.broadcast_to(value[None], (length, *value.shape)), axis, 0, 0, tiled=True
    )


def taken_together(value, axis):
    return copy_for_each(value, axis).sum(axis=0)


def block_parts(c_block, b_block, dt_block, decay_block, reset_block):
    block_len = c_block.shape[0]
    running = jnp.cumsum(decay_block, axis=0)
    reset_count = jnp.cumsum(reset_block, axis=0)
    scores = lax.dot_general(
        c_block, b_block, (((1,), (1,)), ((), ())), preferred_element_type=jnp.float32
    )
    indices = jnp.arange(block_len, dtype=jnp.int32)
    allowed = (indices[:, None] >= indices[None, :]) & (
        reset_count[:, None] == reset_count[None, :]
    )
    log_gap = running.T[:, :, None] - running.T[:, None, :]
    mixing = (
        jnp.where(allowed[None], jnp.exp(jnp.minimum(log_gap, 0.0)), 0.0)
        * scores[None]
        * dt_block.T[:, None, :]
    )
    mixing = mixing.astype(jnp.bfloat16)
    end_count = reset_count[-1]
    carry_weight = jnp.where((reset_count == 0)[:, None], jnp.exp(running), 0.0)
    tail_weight = jnp.where(
        (reset_count == end_count)[:, None], jnp.exp(running[-1][None, :] - running), 0.0
    )
    block_decay = jnp.where(end_count == 0, jnp.exp(running[-1]), 0.0)
    return (mixing, carry_weight, tail_weight, block_decay)


def chain_link(earlier, later):
    return (earlier[0] * later[0], later[0][:, None, None] * earlier[1] + later[1])


def local(
    ssm_input,
    gate_z,
    b_proj,
    c_proj,
    step_size,
    log_decay,
    skip_d,
    norm_gain,
    w_out,
    d_out,
    game_lengths,
):
    seq_len = ssm_input.shape[1]
    local_width = ssm_input.shape[2]
    heads_here = step_size.shape[2]
    head_dim = local_width // heads_here
    state_dim = b_proj.shape[2]
    block_len = min(512, seq_len)
    count_blocks = seq_len // block_len
    total_width = local_width * lax.axis_size("chan")
    x_heads = ssm_input[0].reshape(seq_len, heads_here, head_dim)
    c_rows = c_proj[0]
    b_rows = b_proj[0]
    dt_rows = step_size[0]
    lengths = game_lengths[0]
    starts = jnp.cumsum(lengths) - lengths
    sequence_positions = lax.axis_index(SEQ) * seq_len + jnp.arange(seq_len, dtype=jnp.int32)
    resets = jnp.any(sequence_positions[:, None] == starts[None, :], axis=1).astype(jnp.int32)

    def blocked(array):
        return array.reshape((count_blocks, block_len) + array.shape[1:])

    zero_state = jnp.zeros((heads_here, state_dim, head_dim), jnp.float32)
    unit_decay = jnp.ones((heads_here,), jnp.float32)

    def forward_step(state_pair, block_inputs):
        local_state, before = state_pair
        x_block, c_block, b_block, dt_block, decay_block, reset_block = block_inputs
        mixing, carry_weight, tail_weight, block_decay = block_parts(
            c_block, b_block, dt_block, decay_block, reset_block
        )
        inside = jnp.einsum("hts,shp->thp", mixing, x_block, preferred_element_type=jnp.float32)
        carried = carry_weight[:, :, None] * jnp.einsum(
            "tn,hnp->thp", c_block.astype(jnp.float32), local_state
        )
        scaled = ((tail_weight * dt_block)[:, :, None] * x_block).astype(jnp.bfloat16)
        fresh_state = jnp.einsum("sn,shp->hnp", b_block, scaled, preferred_element_type=jnp.float32)
        new_pair = (block_decay[:, None, None] * local_state + fresh_state, before * block_decay)
        return (
            new_pair,
            (
                inside + carried,
                carry_weight * before[None, :],
                mixing,
                carry_weight,
                tail_weight,
                block_decay,
            ),
        )

    forward_inputs = (
        blocked(x_heads),
        blocked(c_rows),
        blocked(b_rows),
        blocked(dt_rows),
        blocked(log_decay[0]),
        blocked(resets),
    )
    (dev_state, dev_decay), (
        ssd_blocks,
        incoming_weight,
        mixings,
        carry_weights,
        tail_weights,
        block_decays,
    ) = lax.scan(forward_step, (zero_state, unit_decay), forward_inputs)
    _, incoming = prefix_by_axis(
        (dev_decay, dev_state), SEQ, chain_link, (unit_decay, zero_state), False
    )
    from_left = jnp.einsum("tn,hnp->thp", c_rows.astype(jnp.float32), incoming)
    ssd_out = (
        ssd_blocks.reshape(seq_len, heads_here, head_dim)
        + incoming_weight.reshape(seq_len, heads_here)[:, :, None] * from_left
    )
    ssd_out = ssd_out + skip_d[None, :, None] * x_heads.astype(jnp.float32)
    gate_act = jax.nn.silu(gate_z[0].astype(jnp.float32))
    gated = ssd_out.reshape(seq_len, local_width) * gate_act
    square_total = lax.psum(jnp.sum(gated * gated, axis=1), "chan")
    inv_rms = lax.rsqrt(square_total / total_width + NORM_EPS)
    normed = (gated * norm_gain).astype(jnp.bfloat16)
    w_cols = w_out
    projected = sent_and_summed(
        lax.dot_general(
            w_cols, normed, (((0,), (1,)), ((), ())), preferred_element_type=jnp.float32
        ).astype(jnp.bfloat16),
        "chan",
        0,
    ).T
    out = (inv_rms[:, None] * projected).astype(jnp.bfloat16)[None]
    cotangent = d_out[0]
    w_cols = w_out
    pulled = lax.dot_general(
        lax.all_gather(cotangent, "chan", axis=1, tiled=True),
        w_cols,
        (((1,), (1,)), ((), ())),
        preferred_element_type=jnp.float32,
    )
    out_dot = lax.psum(jnp.sum(cotangent.astype(jnp.float32) * projected, axis=1), "chan")
    d_normed = inv_rms[:, None] * pulled
    gain_local = jnp.sum(gated * d_normed, axis=0)
    d_ssd = (
        (norm_gain * d_normed - (inv_rms**3 * out_dot / total_width)[:, None] * gated) * gate_act
    ).astype(jnp.bfloat16)
    d_heads = d_ssd.reshape(seq_len, heads_here, head_dim)
    skip_local = jnp.sum(d_heads.astype(jnp.float32) * x_heads.astype(jnp.float32), axis=(0, 2))
    grad_gain, grad_skip = (taken_together(gain_local, SEQ_DP), taken_together(skip_local, SEQ_DP))

    def backward_step(state_pair, block_inputs):
        local_adjoint, later_decay = state_pair
        d_block, c_block, b_block, dt_block, mixing, carry_weight, tail_weight, block_decay = (
            block_inputs
        )
        inside = jnp.einsum("hts,thp->shp", mixing, d_block, preferred_element_type=jnp.float32)
        carried = (dt_block * tail_weight)[:, :, None] * jnp.einsum(
            "sn,hnp->shp", b_block.astype(jnp.float32), local_adjoint
        )
        weighted = (carry_weight[:, :, None] * d_block).astype(jnp.bfloat16)
        fresh_adjoint = jnp.einsum(
            "tn,thp->hnp", c_block, weighted, preferred_element_type=jnp.float32
        )
        new_pair = (
            fresh_adjoint + block_decay[:, None, None] * local_adjoint,
            later_decay * block_decay,
        )
        return (new_pair, (inside + carried, dt_block * tail_weight * later_decay[None, :]))

    backward_inputs = (
        blocked(d_heads),
        blocked(c_rows),
        blocked(b_rows),
        blocked(dt_rows),
        mixings,
        carry_weights,
        tail_weights,
        block_decays,
    )
    (dev_adjoint, _), (grad_blocks, outgoing_weight) = lax.scan(
        backward_step, (zero_state, unit_decay), backward_inputs, reverse=True
    )
    _, from_right = prefix_by_axis(
        (dev_decay, dev_adjoint), SEQ, chain_link, (unit_decay, zero_state), True
    )
    right_terms = jnp.einsum("sn,hnp->shp", b_rows.astype(jnp.float32), from_right)
    grad_heads = (
        grad_blocks.reshape(seq_len, heads_here, head_dim)
        + outgoing_weight.reshape(seq_len, heads_here)[:, :, None] * right_terms
    )
    grad_heads = grad_heads + skip_d[None, :, None] * d_heads.astype(jnp.float32)
    grad_x = grad_heads.astype(jnp.bfloat16).reshape(1, seq_len, local_width)
    return (out, grad_x, grad_gain, grad_skip)


def solution(mesh):
    finer = Mesh(
        mesh.devices.reshape(4, 8, mesh.shape["chan"], mesh.shape["dp"]),
        ("seq_0", "seq_1", "chan", "dp"),
    )
    return jax.shard_map(
        local,
        mesh=finer,
        in_specs=(
            P("dp", SEQ, "chan"),
            P("dp", SEQ, "chan"),
            P("dp", SEQ, None),
            P("dp", SEQ, None),
            P("dp", SEQ, "chan"),
            P("dp", SEQ, "chan"),
            P("chan"),
            P("chan"),
            P("chan", None),
            P("dp", SEQ, "chan"),
            P("dp", None),
        ),
        out_specs=(P("dp", SEQ, "chan"), P("dp", SEQ, "chan"), P("chan"), P("chan")),
        check_vma=False,
    )
```

profile of v0, /device:TPU:8, one launch (start us, length us, event | category | flops | bytes accessed | tf_op | source)
XLA Modules:
  0.0 205.9 jit_solution(17596666255649511182)
XLA Ops:
  7.2 0.0 all-gather.9.cloned.1.call-start
  7.3 1.0 reduce-window_clone.1
  8.3 0.7 subtract_bitcast_fusion
  8.9 0.1 compare_reduce_fusion
  9.0 0.1 copy.85
  9.1 0.2 broadcast_in_dim.163
  9.3 0.5 slice.212
  9.8 0.1 reduce.5
  10.6 0.8 copy.86
  11.4 0.2 reduce_window_sum.27
  11.6 0.7 broadcast_compare_fusion.1
  12.2 0.8 copy.89
  13.0 0.1 exponential_select_fusion
  13.2 0.1 copy.94
  13.4 0.9 fusion.16
  14.3 0.1 copy.95
  14.4 0.8 fusion.14
  15.3 19.1 %all-gather.3 = bf16[8,1,8]{2,1,0:T(2,128)(2,1)S(1)} all-gather(bf16[1,1,8]{2,1,0:T(2,128)(2,1)S(1)} %get-tuple-element.116), channel_id=1, replica_groups=mesh['seq_0'=4,'seq_1'=8,'chan'=8,'dp'=2] {'seq_1'}, dimensions={0}, use_global_device_ids=true | all-gather | bytes 144 | tf_op jit(solution)/shard_map/all_gather | solution.py:24
  34.4 0.5 convert_bitcast_fusion.2
  34.9 7.0 %all-gather.4 = bf16[4,1,8]{2,1,0:T(2,128)(2,1)S(1)} all-gather(bf16[1,1,8]{2,1,0:T(2,128)(2,1)S(1)} %get-tuple-element.121), channel_id=1, replica_groups=mesh['seq_0'=4,'seq_1'=8,'chan'=8,'dp'=2] {'seq_0'}, dimensions={0}, use_global_device_ids=true | all-gather | bytes 80 | tf_op jit(solution)/shard_map/all_gather | solution.py:24
  41.9 0.1 copy.91
  42.0 0.1 copy.87
  42.1 0.1 copy.96
  42.3 0.5 broadcast_select_fusion.7
  42.8 0.5 fusion.179
  43.4 0.1 fusion.147
  43.5 0.1 fusion.154
  43.6 0.2 fusion.9
  43.8 16.6 %all-gather.9.cloned.1.call-done = bf16[64,128,64]{1,2,0:T(8,128)(2,1)} async-done(((bf16[8,128,64]{1,2,0:T(8,128)(2,1)}), bf16[64,128,64]{1,2,0:T(8,128)(2,1)}) %all-gather.9.cloned.1.call-update) | async-done | bytes 1048592 | tf_op jit(solution)/shard_map/all_gather | solution.py:24
  60.5 1.6 fusion.79
  62.1 13.1 %all_gather.41 = bf16[4,8,128,64]{2,3,1,0:T(8,128)(2,1)S(1)} all-gather(bf16[1,8,128,64]{2,3,1,0:T(8,128)(2,1)S(1)} %fusion.79), channel_id=1, replica_groups=mesh['seq_0'=4,'seq_1'=8,'chan'=8,'dp'=2] {'seq_0'}, dimensions={0}, use_global_device_ids=true | all-gather | bytes 655360 | tf_op jit(solution)/shard_map/all_gather | solution.py:24
  75.2 1.9 fusion.8
  77.2 0.9 multiply_reduce_fusion.1
  78.1 0.8 copy.97
  79.0 1.4 convolution_convert_fusion
  80.4 0.8 copy.110
  81.2 7.6 %all-to-all-start = ((bf16[8,256,128]{1,2,0:T(8,128)(2,1)}), bf16[8,256,128]{1,2,0:T(8,128)(2,1)S(1)}, u32[]{:S(2)}, u32[]{:S(2)}) async-start(bf16[8,256,128]{1,2,0:T(8,128)(2,1)} %bitcast.430), calls=%async_computation | async-start | bytes 1048576 | tf_op jit(solution)/shard_map/all_to_all | solution.py:47
  88.9 0.1 copy.100
  89.0 29.6 %all-gather.1 = bf16[1,128,2048]{2,1,0:T(8,128)(2,1)S(1)} all-gather(bf16[1,128,256]{2,1,0:T(8,128)(2,1)S(1)} %copy-done.6), channel_id=3, replica_groups=mesh['seq_0'=4,'seq_1'=8,'chan'=8,'dp'=2] {'chan'}, dimensions={2}, use_global_device_ids=true | all-gather | bytes 589824 | tf_op jit(solution)/shard_map/all_gather | solution.py:196
  118.6 0.1 convert_reduce_fusion
  118.7 0.9 fusion.88
  119.7 16.8 %all-reduce = (f32[128]{0:T(128)S(1)}, f32[128]{0:T(128)S(1)}) all-reduce(f32[128]{0:T(128)} %get-tuple-element.140, f32[128]{0:T(128)S(1)} %fusion.88), channel_id=1, replica_groups=mesh['seq_0'=4,'seq_1'=8,'chan'=8,'dp'=2] {'chan'}, use_global_device_ids=true, to_apply=%region_5.6 | all-reduce | flops 256 | bytes 2048 | tf_op jit(solution)/shard_map/psum | solution.py:181
  136.6 2.0 fusion.18
  138.7 0.1 copy.101
  138.8 0.8 fusion.13
  139.7 9.3 %all-gather.5 = bf16[4,1,8]{2,1,0:T(2,128)(2,1)S(1)} all-gather(bf16[1,1,8]{2,1,0:T(2,128)(2,1)S(1)} %copy-done.28), channel_id=1, replica_groups=mesh['seq_0'=4,'seq_1'=8,'chan'=8,'dp'=2] {'seq_0'}, dimensions={0}, use_global_device_ids=true | all-gather | bytes 80 | tf_op jit(solution)/shard_map/all_gather | solution.py:24
  149.0 0.2 fusion.7
  149.2 0.1 reduce_sum.76
  149.3 0.1 reduce_sum.77
  149.4 0.6 broadcast_in_dim.174
  150.0 6.1 %all-to-all-start.2 = ((f32[64,1,8]{2,1,0:T(1,128)}), f32[64,1,8]{2,1,0:T(1,128)S(1)}, u32[]{:S(2)}, u32[]{:S(2)}) async-start(f32[64,1,8]{2,1,0:T(1,128)} %broadcast_in_dim.174), calls=%async_computation.2 | async-start | bytes 65536 | tf_op jit(solution)/shard_map/all_to_all | solution.py:53
  156.1 8.5 %all-to-all-done.2 = f32[64,1,8]{2,1,0:T(1,128)S(1)} async-done(((f32[64,1,8]{2,1,0:T(1,128)}), f32[64,1,8]{2,1,0:T(1,128)S(1)}, u32[]{:S(2)}, u32[]{:S(2)}) %all-to-all-start.2) | async-done | bytes 2080 | tf_op jit(solution)/shard_map/all_to_all | solution.py:53
  164.6 0.7 broadcast_in_dim.173
  165.3 5.4 %all-to-all-start.1 = ((f32[64,1,512]{2,1,0:T(1,128)}), f32[64,1,512]{2,1,0:T(1,128)S(1)}, u32[]{:S(2)}, u32[]{:S(2)}) async-start(f32[64,1,512]{2,1,0:T(1,128)} %broadcast_in_dim.173), calls=%async_computation.1 | async-start | bytes 262144 | tf_op jit(solution)/shard_map/all_to_all | solution.py:53
  170.8 0.1 copy.99
  170.9 0.7 fusion.145
  171.6 0.6 reduce_sum.78
  172.2 8.5 %all-to-all-done.1 = f32[64,1,512]{2,1,0:T(1,128)S(1)} async-done(((f32[64,1,512]{2,1,0:T(1,128)}), f32[64,1,512]{2,1,0:T(1,128)S(1)}, u32[]{:S(2)}, u32[]{:S(2)}) %all-to-all-start.1) | async-done | bytes 131104 | tf_op jit(solution)/shard_map/all_to_all | solution.py:53
  180.7 0.7 reduce_sum.74
  181.5 1.6 fusion.62
  183.1 12.8 %all_gather.46 = bf16[4,8,128,64]{2,3,1,0:T(8,128)(2,1)S(1)} all-gather(bf16[1,8,128,64]{2,3,1,0:T(8,128)(2,1)S(1)} %fusion.62), channel_id=1, replica_groups=mesh['seq_0'=4,'seq_1'=8,'chan'=8,'dp'=2] {'seq_0'}, dimensions={0}, use_global_device_ids=true | all-gather | bytes 655360 | tf_op jit(solution)/shard_map/all_gather | solution.py:24
  195.9 1.9 fusion.6
  197.9 0.4 fusion.12
  198.3 0.8 copy.104
  (86 shorter events, 0.5 us)
Async XLA Ops:
  7.2 71.8 %copy-start = (bf16[512,2048]{1,0:T(8,128)(2,1)S(1)}, bf16[512,2048]{1,0:T(8,128)(2,1)}, u32[]{:S(2)}) copy-start(bf16[512,2048]{1,0:T(8,128)(2,1)} %param.19) | copy-start | bytes 6291460
  7.2 34.7 %copy-start.1 = (bf16[1,128,512]{2,1,0:T(8,128)(2,1)S(1)}, bf16[1,128,512]{2,1,0:T(8,128)(2,1)}, u32[]{:S(2)}) copy-start(bf16[1,128,512]{2,1,0:T(8,128)(2,1)} %param.11) | copy-start | bytes 393220
  7.2 7.2 %copy-start.4 = (bf16[1,128,128]{2,1,0:T(8,128)(2,1)S(1)}, bf16[1,128,128]{2,1,0:T(8,128)(2,1)}, u32[]{:S(2)}) copy-start(bf16[1,128,128]{2,1,0:T(8,128)(2,1)} %param.13) | copy-start | bytes 98308
  7.2 34.9 %copy-start.7 = (bf16[1,128,512]{2,1,0:T(8,128)(2,1)S(1)}, bf16[1,128,512]{2,1,0:T(8,128)(2,1)}, u32[]{:S(2)}) copy-start(bf16[1,128,512]{2,1,0:T(8,128)(2,1)} %param.12) | copy-start | bytes 393220
  7.2 36.3 %copy-start.2 = (bf16[1,128,128]{2,1,0:T(8,128)(2,1)S(1)}, bf16[1,128,128]{2,1,0:T(8,128)(2,1)}, u32[]{:S(2)}) copy-start(bf16[1,128,128]{2,1,0:T(8,128)(2,1)} %param.14) | copy-start | bytes 98308
  7.2 53.2 %all-gather.9.cloned.1.call-start = ((), (), s32[]{:S(2)}) async-start(), calls=%async_computation.3 | async-start | bytes 1179648 | tf_op jit(solution)/shard_map/all_gather | solution.py:24
  11.6 30.3 %copy-start.24 = (f32[8]{0:T(128)}, f32[8]{0:T(128)S(1)}, u32[]{:S(2)}) copy-start(f32[8]{0:T(128)S(1)} %fusion.160) | copy-start | bytes 100
  42.1 35.1 %copy-start.22 = (f32[8,128]{1,0:T(8,128)}, f32[8,128]{1,0:T(8,128)S(1)}, u32[]{:S(2)}) copy-start(f32[8,128]{1,0:T(8,128)S(1)} %copy.87) | copy-start | bytes 12292
  43.4 33.8 %copy-start.12 = (f32[8]{0:T(128)}, f32[8]{0:T(128)S(1)}, u32[]{:S(2)}) copy-start(f32[8]{0:T(128)S(1)} %get-tuple-element.125) | copy-start | bytes 100
  43.4 33.8 %copy-start.14 = (f32[8]{0:T(128)}, f32[8]{0:T(128)S(1)}, u32[]{:S(2)}) copy-start(f32[8]{0:T(128)S(1)} %get-tuple-element.126) | copy-start | bytes 100
  43.4 33.8 %copy-start.16 = (f32[8]{0:T(128)}, f32[8]{0:T(128)S(1)}, u32[]{:S(2)}) copy-start(f32[8]{0:T(128)S(1)} %get-tuple-element.127) | copy-start | bytes 100
  43.4 33.8 %copy-start.18 = (f32[8]{0:T(128)}, f32[8]{0:T(128)S(1)}, u32[]{:S(2)}) copy-start(f32[8]{0:T(128)S(1)} %get-tuple-element.128) | copy-start | bytes 100
  43.5 33.7 %copy-start.10 = (pred[128,128]{1,0:T(8,128)(4,1)}, pred[128,128]{1,0:T(8,128)(4,1)S(1)}, u32[]{:S(2)}) copy-start(pred[128,128]{1,0:T(8,128)(4,1)S(1)} %fusion.147) | copy-start | bytes 49156
  43.6 33.6 %copy-start.8 = (f32[128,128]{1,0:T(8,128)}, f32[128,128]{1,0:T(8,128)S(1)}, u32[]{:S(2)}) copy-start(f32[128,128]{1,0:T(8,128)S(1)} %fusion.154) | copy-start | bytes 196612
  75.2 2.0 copy-start.20
  75.2 2.0 copy-start.31
  77.2 1.8 copy-start.30
  80.4 8.6 %copy-start.6 = (bf16[1,128,256]{2,1,0:T(8,128)(2,1)S(1)}, bf16[1,128,256]{2,1,0:T(8,128)(2,1)}, u32[]{:S(2)}) copy-start(bf16[1,128,256]{2,1,0:T(8,128)(2,1)} %param.20) | copy-start | bytes 196612
  81.2 37.4 %all-to-all-start = ((bf16[8,256,128]{1,2,0:T(8,128)(2,1)}), bf16[8,256,128]{1,2,0:T(8,128)(2,1)S(1)}, u32[]{:S(2)}, u32[]{:S(2)}) async-start(bf16[8,256,128]{1,2,0:T(8,128)(2,1)} %bitcast.430), calls=%async_computation | async-start | bytes 1048576 | tf_op jit(solution)/shard_map/all_to_all | solution.py:47
  88.8 92.6 %all-gather.11.cloned.1.call-start = ((), (), s32[]{:S(2)}) async-start(), calls=%async_computation.4 | async-start | bytes 1179648 | tf_op jit(solution)/shard_map/all_gather | solution.py:24
  136.5 2.3 %copy-start.3 = (bf16[1,128,128]{2,1,0:T(8,128)(2,1)S(1)}, bf16[1,128,128]{2,1,0:T(8,128)(2,1)}, u32[]{:S(2)}) copy-start(bf16[1,128,128]{2,1,0:T(8,128)(2,1)} %param.14) | copy-start | bytes 98308
  136.5 2.3 %copy-start.25 = (f32[8]{0:T(128)S(1)}, f32[8]{0:T(128)}, u32[]{:S(2)}) copy-start(f32[8]{0:T(128)} %copy-done.24) | copy-start | bytes 100
  136.5 3.1 %copy-start.28 = (bf16[1,1,8]{2,1,0:T(2,128)(2,1)S(1)}, bf16[1,1,8]{2,1,0:T(2,128)(2,1)}, u32[]{:S(2)}) copy-start(bf16[1,1,8]{2,1,0:T(2,128)(2,1)} %get-tuple-element.120) | copy-start | bytes 52
  136.5 12.5 %copy-start.5 = (bf16[1,128,128]{2,1,0:T(8,128)(2,1)S(1)}, bf16[1,128,128]{2,1,0:T(8,128)(2,1)}, u32[]{:S(2)}) copy-start(bf16[1,128,128]{2,1,0:T(8,128)(2,1)} %param.13) | copy-start | bytes 98308
  138.5 42.9 %copy-start.13 = (f32[8]{0:T(128)S(1)}, f32[8]{0:T(128)}, u32[]{:S(2)}) copy-start(f32[8]{0:T(128)} %copy-done.12) | copy-start | bytes 100
  138.6 42.9 %copy-start.15 = (f32[8]{0:T(128)S(1)}, f32[8]{0:T(128)}, u32[]{:S(2)}) copy-start(f32[8]{0:T(128)} %copy-done.14) | copy-start | bytes 100
  138.6 42.9 %copy-start.17 = (f32[8]{0:T(128)S(1)}, f32[8]{0:T(128)}, u32[]{:S(2)}) copy-start(f32[8]{0:T(128)} %copy-done.16) | copy-start | bytes 100
  138.6 42.9 %copy-start.19 = (f32[8]{0:T(128)S(1)}, f32[8]{0:T(128)}, u32[]{:S(2)}) copy-start(f32[8]{0:T(128)} %copy-done.18) | copy-start | bytes 100
  138.6 42.9 %copy-start.26 = (f32[8]{0:T(128)S(1)}, f32[8]{0:T(128)}, u32[]{:S(2)}) copy-start(f32[8]{0:T(128)} %get-tuple-element.119) | copy-start | bytes 100
  138.6 42.9 %copy-start.27 = (f32[8]{0:T(128)S(1)}, f32[8]{0:T(128)}, u32[]{:S(2)}) copy-start(f32[8]{0:T(128)} %get-tuple-element.122) | copy-start | bytes 100
  138.6 57.3 %copy-start.29 = (f32[8]{0:T(128)S(1)}, f32[8]{0:T(128)}, u32[]{:S(2)}) copy-start(f32[8]{0:T(128)} %get-tuple-element.117) | copy-start | bytes 100
  150.0 14.6 %all-to-all-start.2 = ((f32[64,1,8]{2,1,0:T(1,128)}), f32[64,1,8]{2,1,0:T(1,128)S(1)}, u32[]{:S(2)}, u32[]{:S(2)}) async-start(f32[64,1,8]{2,1,0:T(1,128)} %broadcast_in_dim.174), calls=%async_computation.2 | async-start | bytes 65536 | tf_op jit(solution)/shard_map/all_to_all | solution.py:53
  165.3 15.4 %all-to-all-start.1 = ((f32[64,1,512]{2,1,0:T(1,128)}), f32[64,1,512]{2,1,0:T(1,128)S(1)}, u32[]{:S(2)}, u32[]{:S(2)}) async-start(f32[64,1,512]{2,1,0:T(1,128)} %broadcast_in_dim.173), calls=%async_computation.1 | async-start | bytes 262144 | tf_op jit(solution)/shard_map/all_to_all | solution.py:53
  195.9 2.0 copy-start.9
  195.9 2.0 copy-start.11
  195.9 2.0 copy-start.21
  195.9 2.0 copy-start.23
  195.9 2.0 copy-start.32
Sparse Core Ops, SparseCore 0:
  15.4 45.0 all-gather.8
  139.8 38.7 all-gather.10
where the time goes:
time: 207 us; the launch traced here: 206 us
  blocking collectives  108 us (52%)
  waiting for transfers between devices  33.7 us (16%)
  starting transfers between devices  19.1 us (9%)
  between operations  15.3 us (7%)
  other arithmetic  12 us (6%)
  matrix products  10.7 us (5%)
  local copies, waits for them, and re-layouts  7.31 us (4%)
    all_gather x5, blocking collectives, prefix_by_axis(): lax.all_gather(part.astype(kind), axis)  61.2 us
    all_gather x1, blocking collectives, local(): lax.all_gather(cotangent, 'chan', axis=1, tiled=True)  29.6 us
    all_to_all x2, waiting for transfers between devices, copy_for_each(): lax.all_to_all(jnp.broadcast_to(value[None], (length, *value.shape)), axi...  17.1 us
    psum x1, blocking collectives, local(): square_total = lax.psum(jnp.sum(gated * gated, axis=1), 'chan')  16.8 us
    all_gather x2, waiting for transfers between devices, prefix_by_axis(): lax.all_gather(part.astype(kind), axis)  16.6 us
    all_to_all x2, starting transfers between devices, copy_for_each(): lax.all_to_all(jnp.broadcast_to(value[None], (length, *value.shape)), axi...  11.4 us
    all_to_all x1, starting transfers between devices, sent_and_summed(): lax.all_to_all(in_blocks(value, dim, length), axis, 0, 0, tiled=True)  7.55 us
  transfers between devices with their start and end apart: 5, of which 3 were waited for; matrix products, arithmetic and copies ran while one was open for 3% of the time, Pallas kernels for 0%

commit v1 on v0

--- a/solution.py
+++ b/solution.py
@@ -7,6 +7,23 @@
 SEQ = ("seq_0", "seq_1")
 SEQ_DP = ("seq_0", "seq_1", "dp")
 NORM_EPS = 1e-05
+
+
+def joined_along(parts, dim):
+    parts = jnp.moveaxis(parts, 0, dim)
+    shape = parts.shape
+    return parts.reshape(*shape[:dim], shape[dim] * shape[dim + 1], *shape[dim + 2 :])
+
+
+def ring_gather(array, axis, dim):
+    size = lax.axis_size(axis)
+    forward = [(i, (i + 1) % size) for i in range(size)]
+    blocks = [array]
+    while len(blocks) < size:
+        blocks.append(lax.ppermute(blocks[-1], axis, forward))
+    position = lax.axis_index(axis)
+    blocks = jnp.stack(blocks)[(position - jnp.arange(size)) % size]
+    return joined_along(blocks, dim)
 
 
 def filled_with(value, identity):
@@ -193,7 +210,7 @@
     cotangent = d_out[0]
     w_cols = w_out
     pulled = lax.dot_general(
-        lax.all_gather(cotangent, "chan", axis=1, tiled=True),
+        ring_gather(cotangent, "chan", 1),
         w_cols,
         (((1,), (1,)), ((), ())),
         preferred_element_type=jnp.float32,

time: 207 us -> 210 us (1.014)
  blocking collectives: 108 us -> 72 us
  starting transfers between devices: 19.1 us -> 40.3 us
  local copies, waits for them, and re-layouts: 7.31 us -> 17.4 us
  waiting for transfers between devices: 33.7 us -> 40.9 us
    all_gather x1 -> x0, blocking collectives: 29.6 us -> none  [local(): lax.all_gather(cotangent, 'chan', axis=1, tiled=True)]
    ppermute x0 -> x7, waiting for transfers between devices: none -> 23.8 us  [ring_gather(): blocks.append(lax.ppermute(blocks[-1], axis, forward))]
    ppermute x0 -> x7, starting transfers between devices: none -> 20.1 us  [ring_gather(): blocks.append(lax.ppermute(blocks[-1], axis, forward))]
    all_gather x2, waiting for transfers between devices: 16.6 us -> 0.02 us  [prefix_by_axis(): lax.all_gather(part.astype(kind), axis)]
    unnamed x69 -> x78, local copies, waits for them, and re-layouts: 1.84 us -> 8.8 us
    all_gather x5, blocking collectives: 61.2 us -> 57.6 us  [prefix_by_axis(): lax.all_gather(part.astype(kind), axis)]
    all_to_all x2, starting transfers between devices: 11.4 us -> 14 us  [copy_for_each(): lax.all_to_all(jnp.broadcast_to(value[None], (length, *value.shape)), axi...]
    psum x1, blocking collectives: 16.8 us -> 14.4 us  [local(): square_total = lax.psum(jnp.sum(gated * gated, axis=1), 'chan')]
  transfers between devices with their start and end apart: 5 -> 12, of which waited for: 3 -> 7; matrix products, arithmetic and copies ran while one was open for 3% -> 11% of each run, Pallas kernels for 0% -> 0%
where the time goes in v1:
time: 210 us; the launch traced here: 209 us
  blocking collectives  72 us (34%)
  waiting for transfers between devices  40.9 us (19%)
  starting transfers between devices  40.3 us (19%)
  local copies, waits for them, and re-layouts  17.4 us (8%)
  between operations  15.5 us (7%)
  other arithmetic  12.7 us (6%)
  matrix products  10 us (5%)
    all_gather x5, blocking collectives, prefix_by_axis(): lax.all_gather(part.astype(kind), axis)  57.6 us
    ppermute x7, waiting for transfers between devices, ring_gather(): blocks.append(lax.ppermute(blocks[-1], axis, forward))  23.8 us
    ppermute x7, starting transfers between devices, ring_gather(): blocks.append(lax.ppermute(blocks[-1], axis, forward))  20.1 us
    all_to_all x2, waiting for transfers between devices, copy_for_each(): lax.all_to_all(jnp.broadcast_to(value[None], (length, *value.shape)), axi...  17 us
    psum x1, blocking collectives, local(): square_total = lax.psum(jnp.sum(gated * gated, axis=1), 'chan')  14.4 us
    all_to_all x2, starting transfers between devices, copy_for_each(): lax.all_to_all(jnp.broadcast_to(value[None], (length, *value.shape)), axi...  14 us
    unnamed x78, local copies, waits for them, and re-layouts  8.8 us
    all_to_all x1, starting transfers between devices, sent_and_summed(): lax.all_to_all(in_blocks(value, dim, length), axis, 0, 0, tiled=True)  6.2 us
  transfers between devices with their start and end apart: 12, of which 7 were waited for; matrix products, arithmetic and copies ran while one was open for 11% of the time, Pallas kernels for 0%

profile of v1, /device:TPU:8, one launch (start us, length us, event | category | flops | bytes accessed | tf_op | source)
XLA Modules:
  0.0 208.8 jit_solution(12837055791836823447)
XLA Ops:
  7.3 1.0 reduce-window_clone.1
  8.3 0.7 subtract_bitcast_fusion
  9.3 0.5 slice.214
  10.6 0.8 copy.106
  11.6 0.7 broadcast_compare_fusion.1
  12.2 0.8 copy.109
  13.4 0.9 fusion.15
  14.5 0.8 fusion.14
  15.3 4.3 %collective-permute-start = (bf16[128,256]{1,0:T(8,128)(2,1)S(1)}, bf16[128,256]{1,0:T(8,128)(2,1)}, u32[]{:S(2)}, u32[]{:S(2)}) collective-permute-start(bf16[128,256]{1,0:T(8,128)(2,1)S(1)} %bitcast.454), channel_id=1, source_target_pairs={{0,2},{2,4},{4,6},{6,8},{8,10},{10,12},{12,14},{14,0},{1,3},{3,5},... | collective-permute-start | bytes 196616 | tf_op jit(solution)/shard_map/ppermute | solution.py:23
  19.6 16.7 %all-gather.2 = bf16[8,1,8]{2,1,0:T(2,128)(2,1)S(1)} all-gather(bf16[1,1,8]{2,1,0:T(2,128)(2,1)S(1)} %get-tuple-element.120), channel_id=1, replica_groups=mesh['seq_0'=4,'seq_1'=8,'chan'=8,'dp'=2] {'seq_1'}, dimensions={0}, use_global_device_ids=true | all-gather | bytes 144 | tf_op jit(solution)/shard_map/all_gather | solution.py:41
  36.3 0.5 convert_bitcast_fusion.2
  36.9 8.3 %all-gather.3 = bf16[4,1,8]{2,1,0:T(2,128)(2,1)S(1)} all-gather(bf16[1,1,8]{2,1,0:T(2,128)(2,1)S(1)} %get-tuple-element.125), channel_id=1, replica_groups=mesh['seq_0'=4,'seq_1'=8,'chan'=8,'dp'=2] {'seq_0'}, dimensions={0}, use_global_device_ids=true | all-gather | bytes 80 | tf_op jit(solution)/shard_map/all_gather | solution.py:41
  45.4 0.7 copy.107
  46.4 0.6 constant_dynamic-update-slice_fusion
  47.0 0.6 broadcast_select_fusion.7
  47.6 0.5 fusion.180
  48.1 0.7 fusion.146
  49.0 0.2 fusion.9
  49.2 4.3 %collective-permute-start.1 = (bf16[128,256]{1,0:T(8,128)(2,1)}, bf16[128,256]{1,0:T(8,128)(2,1)S(1)}, u32[]{:S(2)}, u32[]{:S(2)}) collective-permute-start(bf16[128,256]{1,0:T(8,128)(2,1)} %collective-permute-done), channel_id=1, source_target_pairs={{0,2},{2,4},{4,6},{6,8},{8,10},{10,12},{12,14},{14,0},{1,3},{3,5},... | collective-permute-start | bytes 196616 | tf_op jit(solution)/shard_map/ppermute | solution.py:23
  53.5 1.5 bitcast_dynamic-update-slice_fusion.6
  55.0 5.6 %collective-permute-done.1 = bf16[128,256]{1,0:T(8,128)(2,1)S(1)} collective-permute-done((bf16[128,256]{1,0:T(8,128)(2,1)}, bf16[128,256]{1,0:T(8,128)(2,1)S(1)}, u32[]{:S(2)}, u32[]{:S(2)}) %collective-permute-start.1) | collective-permute-done | bytes 65568 | tf_op jit(solution)/shard_map/ppermute | solution.py:23
  60.5 1.9 collective-permute-start.2
  62.4 0.6 bitcast_dynamic-update-slice_fusion.5
  63.1 4.9 %collective-permute-done.2 = bf16[128,256]{1,0:T(8,128)(2,1)} collective-permute-done((bf16[128,256]{1,0:T(8,128)(2,1)S(1)}, bf16[128,256]{1,0:T(8,128)(2,1)}, u32[]{:S(2)}, u32[]{:S(2)}) %collective-permute-start.2) | collective-permute-done | bytes 65568 | tf_op jit(solution)/shard_map/ppermute | solution.py:23
  68.0 1.9 collective-permute-start.3
  69.9 1.6 fusion.78
  71.6 12.8 %all_gather.38 = bf16[4,8,128,64]{2,3,1,0:T(8,128)(2,1)S(1)} all-gather(bf16[1,8,128,64]{2,3,1,0:T(8,128)(2,1)S(1)} %fusion.78), channel_id=1, replica_groups=mesh['seq_0'=4,'seq_1'=8,'chan'=8,'dp'=2] {'seq_0'}, dimensions={0}, use_global_device_ids=true | all-gather | bytes 655360 | tf_op jit(solution)/shard_map/all_gather | solution.py:41
  84.4 1.9 fusion.8
  86.4 0.9 multiply_reduce_fusion.1
  87.5 0.5 convolution_convert_fusion
  88.0 0.8 copy.131
  88.8 6.2 %all-to-all-start = ((bf16[8,256,128]{1,2,0:T(8,128)(2,1)}), bf16[8,256,128]{1,2,0:T(8,128)(2,1)S(1)}, u32[]{:S(2)}, u32[]{:S(2)}) async-start(bf16[8,256,128]{1,2,0:T(8,128)(2,1)} %bitcast.445), calls=%async_computation | async-start | bytes 1048576 | tf_op jit(solution)/shard_map/all_to_all | solution.py:64
  95.1 1.5 bitcast_dynamic-update-slice_fusion.4
  96.6 3.9 %collective-permute-start.4 = (bf16[128,256]{1,0:T(8,128)(2,1)}, bf16[128,256]{1,0:T(8,128)(2,1)S(1)}, u32[]{:S(2)}, u32[]{:S(2)}) collective-permute-start(bf16[128,256]{1,0:T(8,128)(2,1)} %collective-permute-done.3), channel_id=1, source_target_pairs={{0,2},{2,4},{4,6},{6,8},{8,10},{10,12},{12,14},{14,0},{1,3},{3,5},... | collective-permute-start | bytes 196616 | tf_op jit(solution)/shard_map/ppermute | solution.py:23
  100.4 1.5 bitcast_dynamic-update-slice_fusion.3
  101.9 3.7 %collective-permute-done.4 = bf16[128,256]{1,0:T(8,128)(2,1)S(1)} collective-permute-done((bf16[128,256]{1,0:T(8,128)(2,1)}, bf16[128,256]{1,0:T(8,128)(2,1)S(1)}, u32[]{:S(2)}, u32[]{:S(2)}) %collective-permute-start.4) | collective-permute-done | bytes 65568 | tf_op jit(solution)/shard_map/ppermute | solution.py:23
  105.6 1.9 collective-permute-start.5
  107.5 0.6 bitcast_dynamic-update-slice_fusion.2
  108.2 4.8 %collective-permute-done.5 = bf16[128,256]{1,0:T(8,128)(2,1)S(1)} collective-permute-done((bf16[128,256]{1,0:T(8,128)(2,1)S(1)}, bf16[128,256]{1,0:T(8,128)(2,1)S(1)}, u32[]{:S(2)}, u32[]{:S(2)}) %collective-permute-start.5) | collective-permute-done | bytes 65568 | tf_op jit(solution)/shard_map/ppermute | solution.py:23
  113.0 1.9 collective-permute-start.6
  114.9 0.6 bitcast_dynamic-update-slice_fusion.1
  115.5 4.8 %collective-permute-done.6 = bf16[128,256]{1,0:T(8,128)(2,1)S(1)} collective-permute-done((bf16[128,256]{1,0:T(8,128)(2,1)S(1)}, bf16[128,256]{1,0:T(8,128)(2,1)S(1)}, u32[]{:S(2)}, u32[]{:S(2)}) %collective-permute-start.6) | collective-permute-done | bytes 65568 | tf_op jit(solution)/shard_map/ppermute | solution.py:23
  120.4 0.6 bitcast_dynamic-update-slice_fusion
  121.0 1.6 gather_fusion
  122.7 1.0 copy.119
  123.7 0.9 fusion.88
  124.7 14.4 %all-reduce = (f32[128]{0:T(128)S(1)}, f32[128]{0:T(128)S(1)}) all-reduce(f32[128]{0:T(128)} %get-tuple-element.144, f32[128]{0:T(128)S(1)} %fusion.88), channel_id=1, replica_groups=mesh['seq_0'=4,'seq_1'=8,'chan'=8,'dp'=2] {'chan'}, use_global_device_ids=true, to_apply=%region_5.6 | all-reduce | flops 256 | bytes 2048 | tf_op jit(solution)/shard_map/psum | solution.py:198
  139.1 2.2 %fusion.17 = (f32[512]{0:T(512)S(1)}, bf16[128,512]{1,0:T(8,128)(2,1)S(1)}, f32[512]{0:T(512)S(1)}) fusion(bf16[1,128,512]{2,1,0:T(8,128)(2,1)} %param.11, f32[128,512]{1,0:T(8,128)} %copy-done.7, bf16[1,128,512]{2,1,0:T(8,128)(2,1)} %param.12, f32[128]{0:T(128)S(1)} %get-tuple-element.140, f32[512]{0:T(512)} %param.18, bf16[128,2048]{0,1:T(8,128)(2,1)} %bitcast.450, ...), kind=kOutput, calls=%fused_computation.35 | convolution fusion | flops 269614080 | bytes 3283968 | tf_op jit(solution)/shard_map/dot_general | solution.py:212
  141.6 0.8 fusion.13
  142.4 7.0 %all-gather.4 = bf16[4,1,8]{2,1,0:T(2,128)(2,1)S(1)} all-gather(bf16[1,1,8]{2,1,0:T(2,128)(2,1)S(1)} %copy-done.29), channel_id=1, replica_groups=mesh['seq_0'=4,'seq_1'=8,'chan'=8,'dp'=2] {'seq_0'}, dimensions={0}, use_global_device_ids=true | all-gather | bytes 80 | tf_op jit(solution)/shard_map/all_gather | solution.py:41
  149.8 0.6 broadcast_in_dim.175
  150.4 8.5 %all-to-all-start.2 = ((f32[64,1,8]{2,1,0:T(1,128)}), f32[64,1,8]{2,1,0:T(1,128)S(1)}, u32[]{:S(2)}, u32[]{:S(2)}) async-start(f32[64,1,8]{2,1,0:T(1,128)} %broadcast_in_dim.175), calls=%async_computation.2 | async-start | bytes 65536 | tf_op jit(solution)/shard_map/all_to_all | solution.py:70
  159.0 8.5 %all-to-all-done.2 = f32[64,1,8]{2,1,0:T(1,128)S(1)} async-done(((f32[64,1,8]{2,1,0:T(1,128)}), f32[64,1,8]{2,1,0:T(1,128)S(1)}, u32[]{:S(2)}, u32[]{:S(2)}) %all-to-all-start.2) | async-done | bytes 2080 | tf_op jit(solution)/shard_map/all_to_all | solution.py:70
  167.5 0.7 broadcast_in_dim.174
  168.2 5.5 %all-to-all-start.1 = ((f32[64,1,512]{2,1,0:T(1,128)}), f32[64,1,512]{2,1,0:T(1,128)S(1)}, u32[]{:S(2)}, u32[]{:S(2)}) async-start(f32[64,1,512]{2,1,0:T(1,128)} %broadcast_in_dim.174), calls=%async_computation.1 | async-start | bytes 262144 | tf_op jit(solution)/shard_map/all_to_all | solution.py:70
  173.8 0.7 fusion.144
  174.5 0.6 reduce_sum.78
  175.1 8.5 %all-to-all-done.1 = f32[64,1,512]{2,1,0:T(1,128)S(1)} async-done(((f32[64,1,512]{2,1,0:T(1,128)}), f32[64,1,512]{2,1,0:T(1,128)S(1)}, u32[]{:S(2)}, u32[]{:S(2)}) %all-to-all-start.1) | async-done | bytes 131104 | tf_op jit(solution)/shard_map/all_to_all | solution.py:70
  183.6 0.7 reduce_sum.74
  184.3 1.6 fusion.61
  186.0 12.8 %all_gather.42 = bf16[4,8,128,64]{2,3,1,0:T(8,128)(2,1)S(1)} all-gather(bf16[1,8,128,64]{2,3,1,0:T(8,128)(2,1)S(1)} %fusion.61), channel_id=1, replica_groups=mesh['seq_0'=4,'seq_1'=8,'chan'=8,'dp'=2] {'seq_0'}, dimensions={0}, use_global_device_ids=true | all-gather | bytes 655360 | tf_op jit(solution)/shard_map/all_gather | solution.py:41
  198.8 1.9 fusion.6
  200.8 0.4 fusion.12
  201.2 0.8 copy.125
  (113 shorter events, 2.8 us)
Async XLA Ops:
  7.2 80.3 %copy-start = (bf16[512,2048]{1,0:T(8,128)(2,1)S(1)}, bf16[512,2048]{1,0:T(8,128)(2,1)}, u32[]{:S(2)}) copy-start(bf16[512,2048]{1,0:T(8,128)(2,1)} %param.19) | copy-start | bytes 6291460
  7.2 38.1 %copy-start.1 = (bf16[1,128,512]{2,1,0:T(8,128)(2,1)S(1)}, bf16[1,128,512]{2,1,0:T(8,128)(2,1)}, u32[]{:S(2)}) copy-start(bf16[1,128,512]{2,1,0:T(8,128)(2,1)} %param.11) | copy-start | bytes 393220
  7.2 7.3 %copy-start.4 = (bf16[1,128,128]{2,1,0:T(8,128)(2,1)S(1)}, bf16[1,128,128]{2,1,0:T(8,128)(2,1)}, u32[]{:S(2)}) copy-start(bf16[1,128,128]{2,1,0:T(8,128)(2,1)} %param.13) | copy-start | bytes 98308
  7.2 8.1 %copy-start.6 = (bf16[1,128,256]{2,1,0:T(8,128)(2,1)S(1)}, bf16[1,128,256]{2,1,0:T(8,128)(2,1)}, u32[]{:S(2)}) copy-start(bf16[1,128,256]{2,1,0:T(8,128)(2,1)} %param.20) | copy-start | bytes 196612
  7.2 38.9 %copy-start.8 = (bf16[1,128,512]{2,1,0:T(8,128)(2,1)S(1)}, bf16[1,128,512]{2,1,0:T(8,128)(2,1)}, u32[]{:S(2)}) copy-start(bf16[1,128,512]{2,1,0:T(8,128)(2,1)} %param.12) | copy-start | bytes 393220
  7.2 62.7 %all-gather.8.cloned.1.call-start = ((), (), s32[]{:S(2)}) async-start(), calls=%async_computation.3 | async-start | bytes 1179648 | tf_op jit(solution)/shard_map/all_gather | solution.py:41
  11.6 35.4 %copy-start.25 = (f32[8]{0:T(128)}, f32[8]{0:T(128)S(1)}, u32[]{:S(2)}) copy-start(f32[8]{0:T(128)S(1)} %fusion.159) | copy-start | bytes 100
  13.0 35.8 %copy-start.2 = (bf16[1,128,128]{2,1,0:T(8,128)(2,1)S(1)}, bf16[1,128,128]{2,1,0:T(8,128)(2,1)}, u32[]{:S(2)}) copy-start(bf16[1,128,128]{2,1,0:T(8,128)(2,1)} %param.14) | copy-start | bytes 98308
  15.3 33.9 %collective-permute-start = (bf16[128,256]{1,0:T(8,128)(2,1)S(1)}, bf16[128,256]{1,0:T(8,128)(2,1)}, u32[]{:S(2)}, u32[]{:S(2)}) collective-permute-start(bf16[128,256]{1,0:T(8,128)(2,1)S(1)} %bitcast.454), channel_id=1, source_target_pairs={{0,2},{2,4},{4,6},{6,8},{8,10},{10,12},{12,14},{14,0},{1,3},{3,5},... | collective-permute-start | bytes 196616 | tf_op jit(solution)/shard_map/ppermute | solution.py:23
  48.1 38.2 %copy-start.13 = (f32[8]{0:T(128)}, f32[8]{0:T(128)S(1)}, u32[]{:S(2)}) copy-start(f32[8]{0:T(128)S(1)} %get-tuple-element.129) | copy-start | bytes 100
  48.1 38.2 %copy-start.15 = (f32[8]{0:T(128)}, f32[8]{0:T(128)S(1)}, u32[]{:S(2)}) copy-start(f32[8]{0:T(128)S(1)} %get-tuple-element.130) | copy-start | bytes 100
  48.1 38.2 %copy-start.17 = (f32[8]{0:T(128)}, f32[8]{0:T(128)S(1)}, u32[]{:S(2)}) copy-start(f32[8]{0:T(128)S(1)} %get-tuple-element.131) | copy-start | bytes 100
  48.1 38.2 %copy-start.19 = (f32[8]{0:T(128)}, f32[8]{0:T(128)S(1)}, u32[]{:S(2)}) copy-start(f32[8]{0:T(128)S(1)} %get-tuple-element.132) | copy-start | bytes 100
  49.0 37.4 %copy-start.9 = (f32[128,128]{1,0:T(8,128)}, f32[128,128]{1,0:T(8,128)S(1)}, u32[]{:S(2)}) copy-start(f32[128,128]{1,0:T(8,128)S(1)} %fusion.153) | copy-start | bytes 196612
  49.2 11.3 %collective-permute-start.1 = (bf16[128,256]{1,0:T(8,128)(2,1)}, bf16[128,256]{1,0:T(8,128)(2,1)S(1)}, u32[]{:S(2)}, u32[]{:S(2)}) collective-permute-start(bf16[128,256]{1,0:T(8,128)(2,1)} %collective-permute-done), channel_id=1, source_target_pairs={{0,2},{2,4},{4,6},{6,8},{8,10},{10,12},{12,14},{14,0},{1,3},{3,5},... | collective-permute-start | bytes 196616 | tf_op jit(solution)/shard_map/ppermute | solution.py:23
  60.5 7.5 %collective-permute-start.2 = (bf16[128,256]{1,0:T(8,128)(2,1)S(1)}, bf16[128,256]{1,0:T(8,128)(2,1)}, u32[]{:S(2)}, u32[]{:S(2)}) collective-permute-start(bf16[128,256]{1,0:T(8,128)(2,1)S(1)} %collective-permute-done.1), channel_id=1, source_target_pairs={{0,2},{2,4},{4,6},{6,8},{8,10},{10,12},{12,14},{14,0},{1,3},{3,5},... | collective-permute-start | bytes 196616 | tf_op jit(solution)/shard_map/ppermute | solution.py:23
  68.0 28.6 %collective-permute-start.3 = (bf16[128,256]{1,0:T(8,128)(2,1)}, bf16[128,256]{1,0:T(8,128)(2,1)}, u32[]{:S(2)}, u32[]{:S(2)}) collective-permute-start(bf16[128,256]{1,0:T(8,128)(2,1)} %collective-permute-done.2), channel_id=1, source_target_pairs={{0,2},{2,4},{4,6},{6,8},{8,10},{10,12},{12,14},{14,0},{1,3},{3,5},... | collective-permute-start | bytes 196616 | tf_op jit(solution)/shard_map/ppermute | solution.py:23
  84.4 2.0 copy-start.11
  84.4 2.0 copy-start.21
  84.4 2.0 copy-start.23
  84.4 2.0 copy-start.32
  86.4 1.1 copy-start.31
  87.5 1.3 copy-start.7
  88.8 34.8 %all-to-all-start = ((bf16[8,256,128]{1,2,0:T(8,128)(2,1)}), bf16[8,256,128]{1,2,0:T(8,128)(2,1)S(1)}, u32[]{:S(2)}, u32[]{:S(2)}) async-start(bf16[8,256,128]{1,2,0:T(8,128)(2,1)} %bitcast.445), calls=%async_computation | async-start | bytes 1048576 | tf_op jit(solution)/shard_map/all_to_all | solution.py:64
  95.0 89.3 %all-gather.10.cloned.1.call-start = ((), (), s32[]{:S(2)}) async-start(), calls=%async_computation.4 | async-start | bytes 1179648 | tf_op jit(solution)/shard_map/all_gather | solution.py:41
  96.6 9.1 %collective-permute-start.4 = (bf16[128,256]{1,0:T(8,128)(2,1)}, bf16[128,256]{1,0:T(8,128)(2,1)S(1)}, u32[]{:S(2)}, u32[]{:S(2)}) collective-permute-start(bf16[128,256]{1,0:T(8,128)(2,1)} %collective-permute-done.3), channel_id=1, source_target_pairs={{0,2},{2,4},{4,6},{6,8},{8,10},{10,12},{12,14},{14,0},{1,3},{3,5},... | collective-permute-start | bytes 196616 | tf_op jit(solution)/shard_map/ppermute | solution.py:23
  105.6 7.4 %collective-permute-start.5 = (bf16[128,256]{1,0:T(8,128)(2,1)S(1)}, bf16[128,256]{1,0:T(8,128)(2,1)S(1)}, u32[]{:S(2)}, u32[]{:S(2)}) collective-permute-start(bf16[128,256]{1,0:T(8,128)(2,1)S(1)} %collective-permute-done.4), channel_id=1, source_target_pairs={{0,2},{2,4},{4,6},{6,8},{8,10},{10,12},{12,14},{14,0},{1,3},{3,5},... | collective-permute-start | bytes 196616 | tf_op jit(solution)/shard_map/ppermute | solution.py:23
  113.0 7.4 %collective-permute-start.6 = (bf16[128,256]{1,0:T(8,128)(2,1)S(1)}, bf16[128,256]{1,0:T(8,128)(2,1)S(1)}, u32[]{:S(2)}, u32[]{:S(2)}) collective-permute-start(bf16[128,256]{1,0:T(8,128)(2,1)S(1)} %collective-permute-done.5), channel_id=1, source_target_pairs={{0,2},{2,4},{4,6},{6,8},{8,10},{10,12},{12,14},{14,0},{1,3},{3,5},... | collective-permute-start | bytes 196616 | tf_op jit(solution)/shard_map/ppermute | solution.py:23
  139.1 2.4 %copy-start.3 = (bf16[1,128,128]{2,1,0:T(8,128)(2,1)S(1)}, bf16[1,128,128]{2,1,0:T(8,128)(2,1)}, u32[]{:S(2)}) copy-start(bf16[1,128,128]{2,1,0:T(8,128)(2,1)} %param.14) | copy-start | bytes 98308
  139.1 2.4 %copy-start.26 = (f32[8]{0:T(128)S(1)}, f32[8]{0:T(128)}, u32[]{:S(2)}) copy-start(f32[8]{0:T(128)} %copy-done.25) | copy-start | bytes 100
  139.1 3.3 %copy-start.29 = (bf16[1,1,8]{2,1,0:T(2,128)(2,1)S(1)}, bf16[1,1,8]{2,1,0:T(2,128)(2,1)}, u32[]{:S(2)}) copy-start(bf16[1,1,8]{2,1,0:T(2,128)(2,1)} %get-tuple-element.124) | copy-start | bytes 52
  139.1 10.3 %copy-start.5 = (bf16[1,128,128]{2,1,0:T(8,128)(2,1)S(1)}, bf16[1,128,128]{2,1,0:T(8,128)(2,1)}, u32[]{:S(2)}) copy-start(bf16[1,128,128]{2,1,0:T(8,128)(2,1)} %param.13) | copy-start | bytes 98308
  141.3 43.0 %copy-start.14 = (f32[8]{0:T(128)S(1)}, f32[8]{0:T(128)}, u32[]{:S(2)}) copy-start(f32[8]{0:T(128)} %copy-done.13) | copy-start | bytes 100
  141.3 43.0 %copy-start.16 = (f32[8]{0:T(128)S(1)}, f32[8]{0:T(128)}, u32[]{:S(2)}) copy-start(f32[8]{0:T(128)} %copy-done.15) | copy-start | bytes 100
  141.3 43.0 %copy-start.18 = (f32[8]{0:T(128)S(1)}, f32[8]{0:T(128)}, u32[]{:S(2)}) copy-start(f32[8]{0:T(128)} %copy-done.17) | copy-start | bytes 100
  141.3 43.0 %copy-start.20 = (f32[8]{0:T(128)S(1)}, f32[8]{0:T(128)}, u32[]{:S(2)}) copy-start(f32[8]{0:T(128)} %copy-done.19) | copy-start | bytes 100
  141.4 43.0 %copy-start.27 = (f32[8]{0:T(128)S(1)}, f32[8]{0:T(128)}, u32[]{:S(2)}) copy-start(f32[8]{0:T(128)} %get-tuple-element.123) | copy-start | bytes 100
  141.4 43.0 %copy-start.28 = (f32[8]{0:T(128)S(1)}, f32[8]{0:T(128)}, u32[]{:S(2)}) copy-start(f32[8]{0:T(128)} %get-tuple-element.126) | copy-start | bytes 100
  141.4 57.4 %copy-start.30 = (f32[8]{0:T(128)S(1)}, f32[8]{0:T(128)}, u32[]{:S(2)}) copy-start(f32[8]{0:T(128)} %get-tuple-element.121) | copy-start | bytes 100
  150.4 17.0 %all-to-all-start.2 = ((f32[64,1,8]{2,1,0:T(1,128)}), f32[64,1,8]{2,1,0:T(1,128)S(1)}, u32[]{:S(2)}, u32[]{:S(2)}) async-start(f32[64,1,8]{2,1,0:T(1,128)} %broadcast_in_dim.175), calls=%async_computation.2 | async-start | bytes 65536 | tf_op jit(solution)/shard_map/all_to_all | solution.py:70
  168.2 15.4 %all-to-all-start.1 = ((f32[64,1,512]{2,1,0:T(1,128)}), f32[64,1,512]{2,1,0:T(1,128)S(1)}, u32[]{:S(2)}, u32[]{:S(2)}) async-start(f32[64,1,512]{2,1,0:T(1,128)} %broadcast_in_dim.174), calls=%async_computation.1 | async-start | bytes 262144 | tf_op jit(solution)/shard_map/all_to_all | solution.py:70
  198.8 2.0 copy-start.10
  198.8 2.0 copy-start.12
  198.8 2.0 copy-start.22
  198.8 2.0 copy-start.24
  198.8 2.0 copy-start.33
Sparse Core Ops, SparseCore 0:
  15.4 45.1 all-gather.7
  142.5 38.8 all-gather.9
